TPU v7x, 32 devices: a whole 2x2x4 slice. The times are simulated.
32 devices in a mesh: slab: 8 (over z, y), plane: 4 (over x, core).
Axes of the slice: x: 2, y: 2, z: 4, core: 2. Of those that a mesh axis runs over, the one named last changes fastest.
Arguments:
- a_blocks: bfloat16 [4, 96, 7, 128, 128], P('plane', 'slab'), may hold values from -0.1875 to 0.1875
- a_cols: int32 [4, 96, 7], P('plane', 'slab'), may hold values from 0 to 95, as said below
- p_blocks: bfloat16 [4, 96, 4, 128, 128], P('plane', 'slab'), may hold values from -0.75 to 0.75
- p_cols: int32 [4, 96, 4], replicated, may hold values from 0 to 31, as said below
- coarse_slot: int32 [8, 4], replicated, may hold values from 0 to 3, each once within a row
Outputs:
- coarse_op: float32 [4, 8, 128, 2560], P('plane', 'slab')
Inputs may be any that keep to these rules, and one draw needn't show every extreme that they name: `a_cols`: row g = s*12 + r of column p names 7 distinct block rows of column p, among them g itself; they lie in s*12 to s*12 + 11, or, if r < 4, in the 4 rows just below s*12, or, if r >= 8, in the 4 rows from (s+1)*12 on. `p_cols`: row g = s*12 + r names 4 distinct coarse blocks of s*4 to s*4 + 3, or, if r < 4, also of the 4 blocks before, or, if r >= 8, of the 4 blocks after. `coarse_slot`: each row is a permutation of 0 to 3.
All inputs are finite; a program needn't handle non-finite values.
Results may differ from a plain program's by a relative error of at most 0.0029.
Values may be sent and summed in bfloat16 or wider, within the bound.
A program may use at most 192 MiB of HBM per device.

v0:
```python
import functools

import jax
import jax.numpy as jnp
from jax import lax
from jax.experimental import pallas as pl
from jax.experimental.pallas import tpu as pltpu
from jax.sharding import PartitionSpec as P

GHOST = 4
MESH = pl.DeviceIdType.MESH


def kernel(dims, a_cols_hbm, p_cols_hbm, slots_hbm, a_hbm, p_hbm, out, *scratch):
    slabs, planes, rows, links, kp, block, coarse, owned = dims
    stages = planes.bit_length() - 1
    edge = coarse * block
    width = 3 * edge
    chunks = 3
    (a_own, p_own, p_low, p_high, pt, q, qt0, qt1, qt2, ap, final,
     send_c, recv_c, local_sem, halo_send, halo_recv, c_sem, c_got, table, whole, out_sem, a_cols, p_cols, slots, index_sem) = scratch[:25]
    rest = scratch[25:]
    send_b, recv_b, keep_b, b_sem, b_got = (rest[i * stages : (i + 1) * stages] for i in range(5))
    slab = lax.axis_index("slab")
    me = lax.axis_index("plane")
    bits = [(me // (1 << t)) % 2 for t in range(stages)]
    partners = [me + (1 - 2 * bits[t]) * (1 << t) for t in range(stages)]
    has_low = slab > 0
    has_high = slab < slabs - 1

    copy_a = pltpu.make_async_copy(a_hbm, a_own, local_sem.at[0])
    copy_p = pltpu.make_async_copy(p_hbm, p_own.at[pl.ds(0, rows * kp)], local_sem.at[1])
    copy_index = [
        pltpu.make_async_copy(source, target, index_sem.at[i])
        for i, (source, target) in enumerate(
            ((a_cols_hbm, a_cols), (p_cols_hbm, p_cols), (slots_hbm, slots)))
    ]
    for copy in copy_index:
        copy.start()
    copy_p.start()
    copy_a.start()

    barrier = pltpu.get_barrier_semaphore()
    for t in range(stages):
        pl.semaphore_signal(barrier, inc=1, device_id=(slab, partners[t]), device_id_type=MESH)

    @pl.when(has_low)
    def _():
        pl.semaphore_signal(barrier, inc=1, device_id=(slab - 1, me), device_id_type=MESH)

    @pl.when(has_high)
    def _():
        pl.semaphore_signal(barrier, inc=1, device_id=(slab + 1, me), device_id_type=MESH)

    neighbours = stages + jnp.where(has_low, 1, 0) + jnp.where(has_high, 1, 0)
    pl.semaphore_wait(barrier, neighbours)

    ghosts = GHOST * kp
    halo_up = pltpu.make_async_remote_copy(
        src_ref=p_hbm.at[pl.ds((rows - GHOST) * kp, ghosts)],
        dst_ref=p_low.at[pl.ds(0, ghosts)],
        send_sem=halo_send.at[0], recv_sem=halo_recv.at[0],
        device_id=(slab + 1, me), device_id_type=MESH)
    halo_down = pltpu.make_async_remote_copy(
        src_ref=p_hbm.at[pl.ds(0, ghosts)],
        dst_ref=p_high.at[pl.ds(0, ghosts)],
        send_sem=halo_send.at[1], recv_sem=halo_recv.at[1],
        device_id=(slab - 1, me), device_id_type=MESH)

    @pl.when(has_high)
    def _():
        halo_up.start()

    start = slab * rows
    total = p_cols.shape[2]

    def chart(n, _):
        row = jnp.clip(start - GHOST + n, 0, total - 1)
        place = []
        for m in range(kp):
            col = p_cols[me, m, row]
            near = col // coarse
            place.append((near - slab + 1) * coarse + slots[col % coarse, near])
        low, high = n < GHOST, n >= GHOST + rows
        base = jnp.where(low, n, jnp.where(high, n - GHOST - rows, n - GHOST)) * kp
        none = jnp.where(low | high, GHOST * kp, rows * kp)
        for w in range(3 * coarse):
            value = none
            for m in range(kp):
                value = jnp.where(place[m] == w, base + m, value)
            table[n, w] = value
        return 0

    for copy in copy_index:
        copy.wait()
    lax.fori_loop(0, rows + 2 * GHOST, chart, 0)

    zero = jnp.zeros((block, block), jnp.bfloat16)
    p_own[rows * kp] = zero
    p_low[ghosts] = zero
    p_high[ghosts] = zero

    @pl.when(slab == 0)
    def _():
        p_low[...] = jnp.zeros_like(p_low)
        recv_c[1] = jnp.zeros(recv_c.shape[1:], recv_c.dtype)

    @pl.when(slab == slabs - 1)
    def _():
        p_high[...] = jnp.zeros_like(p_high)
        recv_c[0] = jnp.zeros(recv_c.shape[1:], recv_c.dtype)

    def spread(first, count, blocks):
        def body(i, _):
            n = first + i
            for w in range(3 * coarse):
                q[n, :, w * block : (w + 1) * block] = blocks[table[n, w]]
            return 0

        lax.fori_loop(0, count, body, 0)

    def multiply(first, count, columns):
        def body(i, _):
            g = first + i
            left = jnp.concatenate([a_own[g * links + k] for k in range(links)], axis=1)
            at = [jnp.clip(a_cols[k, 0, g] - (start - GHOST), 0, rows + 2 * GHOST - 1) for k in range(links)]
            for c in columns:
                right = jnp.concatenate(
                    [q[at[k], :, c * edge : (c + 1) * edge] for k in range(links)], axis=0)
                ap[pl.ds(pl.multiple_of(g * block, block), block), c * edge : (c + 1) * edge] = jnp.dot(
                    left, right, preferred_element_type=jnp.float32).astype(jnp.bfloat16)
            return 0

        lax.fori_loop(0, count, body, 0)

    copy_p.wait()
    spread(GHOST, rows, p_own)

    def flip(b, _):
        pt[b] = p_own[b].T
        return 0

    lax.fori_loop(0, rows * kp + 1, flip, 0)
    parts = ((qt0, 0, GHOST), (qt1, 0, rows), (qt2, rows - GHOST, GHOST))
    for j, (qt, first, count) in enumerate(parts):
        for i in range(count):
            for slot in range(coarse):
                qt[slot // owned, (slot % owned) * block : (slot % owned + 1) * block, i * block : (i + 1) * block] = (
                    pt[table[GHOST + first + i, j * coarse + slot]])
    copy_a.wait()
    multiply(GHOST, rows - 2 * GHOST, range(chunks))

    def stage_copy(t, j, c):
        return pltpu.make_async_remote_copy(
            src_ref=send_b[t].at[j, c], dst_ref=recv_b[t].at[j, c],
            send_sem=b_sem[t].at[j, c], recv_sem=b_got[t].at[j, c],
            device_id=(slab, partners[t]), device_id_type=MESH)

    def final_copy(j, c):
        return pltpu.make_async_remote_copy(
            src_ref=send_c.at[j, c], dst_ref=recv_c.at[j, c],
            send_sem=c_sem.at[j, c], recv_sem=c_got.at[j, c],
            device_id=(slab - 1 if j == 0 else slab + 1, me), device_id_type=MESH)

    def form(j, columns):
        qt, first, count = parts[j]
        half = planes // 2
        for c in columns:
            right = ap[first * block : (first + count) * block, c * edge : (c + 1) * edge]
            for i in range(half):
                send_b[0][j, c, i] = jnp.dot(
                    qt[1 - bits[0] + 2 * i], right, preferred_element_type=jnp.float32).astype(jnp.bfloat16)
            stage_copy(0, j, c).start()
            for i in range(half):
                keep_b[0][j, c, i] = jnp.dot(
                    qt[bits[0] + 2 * i], right, preferred_element_type=jnp.float32)

    def fold(t, j):
        for c in range(chunks):
            stage_copy(t - 1, j, c).wait_recv()
            for i in range(planes >> (t + 1)):
                at = 1 - bits[t] + 2 * i
                send_b[t][j, c, i] = (
                    keep_b[t - 1][j, c, at] + recv_b[t - 1][j, c, at].astype(jnp.float32)).astype(jnp.bfloat16)
            stage_copy(t, j, c).start()
            for i in range(planes >> (t + 1)):
                at = bits[t] + 2 * i
                keep_b[t][j, c, i] = keep_b[t - 1][j, c, at] + recv_b[t - 1][j, c, at].astype(jnp.float32)

    def finish(j, which):
        for c in which:
            stage_copy(stages - 1, j, c).wait_recv()
            value = keep_b[stages - 1][j, c, 0] + recv_b[stages - 1][j, c, 0].astype(jnp.float32)
            if j == 1:
                final[c] = value
            else:
                send_c[j // 2, c] = value.astype(jnp.bfloat16)

                @pl.when(has_low if j == 0 else has_high)
                def _():
                    final_copy(j // 2, c).start()

    @pl.when(has_high)
    def _():
        halo_up.wait_send()

    @pl.when(has_low)
    def _():
        halo_down.start()
        halo_up.wait_recv()

    spread(0, GHOST, p_low)
    for c in range(chunks):
        multiply(0, GHOST, (c,))
        form(0, (c,))
    for t in range(1, stages):
        fold(t, 0)
    finish(0, range(chunks - 1))

    @pl.when(has_high)
    def _():
        halo_down.wait_recv()

    spread(GHOST + rows, GHOST, p_high)
    for c in range(chunks):
        multiply(rows - GHOST, GHOST, (c,))
        form(2, (c,))
        if c == 0:
            finish(0, range(chunks - 1, chunks))
    for t in range(1, stages):
        fold(t, 2)
    form(1, range(chunks))
    for t in range(1, stages):
        fold(t, 1)
    finish(2, range(chunks))
    finish(1, range(chunks))

    @pl.when(has_high)
    def _():
        for c in range(chunks):
            final_copy(0, c).wait_recv()

    @pl.when(has_low)
    def _():
        for c in range(chunks):
            final_copy(1, c).wait_recv()

    def out_copy(o):
        return pltpu.make_async_copy(whole.at[o], out.at[:, pl.ds(o * edge, edge)], out_sem.at[o])

    for o in range(5):
        terms = []
        if 0 <= o - 1 < chunks:
            terms.append(final[o - 1])
        if o < chunks:
            terms.append(recv_c[1, o].astype(jnp.float32))
        if o >= 2:
            terms.append(recv_c[0, o - 2].astype(jnp.float32))
        whole[o] = functools.reduce(jnp.add, terms)
        out_copy(o).start()

    @pl.when(has_high)
    def _():
        for c in range(chunks):
            final_copy(1, c).wait_send()

    @pl.when(has_low)
    def _():
        halo_down.wait_send()
        for c in range(chunks):
            final_copy(0, c).wait_send()

    for t in range(stages):
        for j in range(3):
            for c in range(chunks):
                stage_copy(t, j, c).wait_send()
    for o in range(5):
        out_copy(o).wait()


def on_device(a_blocks, a_cols, p_blocks, p_cols, coarse_slot):
    rows, links, block = a_blocks.shape[1:4]
    kp = p_blocks.shape[2]
    coarse = coarse_slot.shape[1]
    slabs = lax.axis_size("slab")
    planes = lax.axis_size("plane")
    owned = coarse // planes
    stages = planes.bit_length() - 1
    assert planes == 1 << stages and stages > 0
    edge = coarse * block
    width = 3 * edge
    high = owned * block
    dims = (slabs, planes, rows, links, kp, block, coarse, owned)
    bf, f32 = jnp.bfloat16, jnp.float32
    vmem = pltpu.VMEM
    dma = pltpu.SemaphoreType.DMA
    shape = lambda t: (3, 3, planes >> (t + 1), high, edge)
    scratch = [
        vmem((rows * links, block, block), bf),
        vmem((rows * kp + 1, block, block), bf),
        vmem((GHOST * kp + 1, block, block), bf),
        vmem((GHOST * kp + 1, block, block), bf),
        vmem((rows * kp + 1, block, block), bf),
        vmem((rows + 2 * GHOST, block, width), bf),
        vmem((planes, high, GHOST * block), bf),
        vmem((planes, high, rows * block), bf),
        vmem((planes, high, GHOST * block), bf),
        vmem((rows * block, width), bf),
        vmem((3, high, edge), f32),
        vmem((2, 3, high, edge), bf),
        vmem((2, 3, high, edge), bf),
        dma((2,)), dma((2,)), dma((2,)), dma((2, 3)), dma((2, 3)),
        pltpu.SMEM((rows + 2 * GHOST, 3 * coarse), jnp.int32),
        vmem((5, high, edge), f32),
        dma((5,)),
        pltpu.SMEM((links, 1, rows), jnp.int32),
        pltpu.SMEM((planes, kp, p_cols.shape[1]), jnp.int32),
        pltpu.SMEM((coarse, slabs), jnp.int32),
        dma((3,)),
    ]
    scratch += [vmem(shape(t), bf) for t in range(stages)]
    scratch += [vmem(shape(t), bf) for t in range(stages)]
    scratch += [vmem(shape(t), f32) for t in range(stages)]
    scratch += [dma((3, 3)) for t in range(2 * stages)]
    outside = pl.BlockSpec(memory_space=pltpu.HBM)
    anywhere = pl.BlockSpec(memory_space=pl.ANY)
    result = pl.pallas_call(
        functools.partial(kernel, dims),
        out_shape=jax.ShapeDtypeStruct((high, 5 * edge), f32),
        in_specs=[outside] * 5,
        out_specs=anywhere,
        scratch_shapes=scratch,
        compiler_params=pltpu.CompilerParams(
            collective_id=0, has_side_effects=True, vmem_limit_bytes=44 * 1024 * 1024),
    )(*(pltpu.with_memory_space_constraint(x, pltpu.HBM) for x in (
        a_cols.transpose(2, 0, 1), p_cols.transpose(0, 2, 1), coarse_slot.T,
        a_blocks.reshape(rows * links, block, block), p_blocks.reshape(rows * kp, block, block))))
    return result.reshape(1, owned, block, 5 * edge)


def solution(mesh):
    return jax.shard_map(
        on_device,
        mesh=mesh,
        in_specs=(
            P("plane", "slab", None, None, None),
            P("plane", "slab", None),
            P("plane", "slab", None, None, None),
            P(),
            P(),
        ),
        out_specs=P("plane", "slab", None, None),
        check_vma=False,
    )
```

profile of v0, /device:TPU:0, one launch (start us, length us, event | category | flops | bytes accessed | tf_op | source)
XLA Modules:
  0.0 54.0 jit_solution(16775328870929858474)
XLA Ops:
  0.0 52.9 %shard_map.55 = f32[128,2560]{1,0:T(8,128)S(1)} custom-call(s32[7,1,12]{2,1,0:T(1,128)} %bitcast.10, s32[4,4,96]{2,1,0:T(4,128)} %bitcast.9, s32[4,8]{1,0:T(4,128)} %bitcast.11, bf16[84,128,128]{2,1,0:T(8,128)(2,1)} %bitcast.7, bf16[48,128,128]{2,1,0:T(8,128)(2,1)} %bitcast.8), custom_call_target="tpu_custom_call" | custom-call | tf_op jit(solution)/shard_map/pallas_call | solution.py:327
  52.9 1.1 %copy.7 = f32[1,1,128,2560]{3,2,1,0:T(8,128)} copy(f32[1,1,128,2560]{3,2,1,0:T(8,128)S(1)} %bitcast.6) | data formatting | bytes 2621440
where the time goes:
time: 54.1 us; the launch traced here: 54 us
  Pallas kernels  52.9 us (98%)
  local copies, waits for them, and re-layouts  1.06 us (2%)
    pallas_call x1, Pallas kernels, on_device(): pl.pallas_call(functools.partial(kernel, dims), out_shape=jax.ShapeDtypeS...  52.9 us

commit v1 on v0

v1 whole, which is shorter than its diff:
```python
import functools

import jax
import jax.numpy as jnp
from jax import lax
from jax.experimental import pallas as pl
from jax.experimental.pallas import tpu as pltpu
from jax.sharding import PartitionSpec as P

GHOST = 4
MESH = pl.DeviceIdType.MESH


def kernel(dims, a_cols_hbm, p_cols_hbm, slots_hbm, a_hbm, p_hbm, out, *scratch):
    slabs, planes, rows, links, kp, block, coarse, owned = dims
    stages = planes.bit_length() - 1
    edge = coarse * block
    chunks = 3
    ghosts = GHOST * kp
    (a_own, p_own, p_low, p_high, q0, q1, q2, qt0, qt1, qt2, dense, dense_low, dense_high, ap, keep_ap, final,
     send_c, recv_c, local_sem, halo_send, halo_recv, c_sem, c_got, whole, out_sem, a_cols, p_cols, slots,
     index_sem) = scratch[:29]
    rest = scratch[29:]
    send_b, recv_b, keep_b, b_sem, b_got = (rest[i * stages : (i + 1) * stages] for i in range(5))
    slab = lax.axis_index("slab")
    me = lax.axis_index("plane")
    bits = [(me // (1 << t)) % 2 for t in range(stages)]
    partners = [me + (1 - 2 * bits[t]) * (1 << t) for t in range(stages)]
    has_low = slab > 0
    has_high = slab < slabs - 1
    f32, bf = jnp.float32, jnp.bfloat16
    start = slab * rows
    total = p_cols.shape[2]
    dot = functools.partial(jnp.dot, preferred_element_type=f32)

    copy_index = [
        pltpu.make_async_copy(source, target, index_sem.at[i])
        for i, (source, target) in enumerate(
            ((a_cols_hbm, a_cols), (p_cols_hbm, p_cols), (slots_hbm, slots)))
    ]
    spans = ((rows - GHOST, GHOST), (0, GHOST), (GHOST, rows - 2 * GHOST))
    copy_p = [
        pltpu.make_async_copy(
            p_hbm.at[pl.ds(first * kp, count * kp)], p_own.at[pl.ds(first * kp, count * kp)], local_sem.at[1 + i])
        for i, (first, count) in enumerate(spans)
    ]
    copy_a = pltpu.make_async_copy(a_hbm, a_own.at[pl.ds(0, rows * links)], local_sem.at[0])
    copy_p[0].start()
    for copy in copy_index:
        copy.start()
    for copy in copy_p[1:]:
        copy.start()
    copy_a.start()

    barrier = pltpu.get_barrier_semaphore()
    for t in range(stages):
        pl.semaphore_signal(barrier, inc=1, device_id=(slab, partners[t]), device_id_type=MESH)

    @pl.when(has_low)
    def _():
        pl.semaphore_signal(barrier, inc=1, device_id=(slab - 1, me), device_id_type=MESH)

    @pl.when(has_high)
    def _():
        pl.semaphore_signal(barrier, inc=1, device_id=(slab + 1, me), device_id_type=MESH)

    zero = jnp.zeros((block, block), bf)
    a_own[rows * links] = zero
    p_own[rows * kp] = zero
    p_low[ghosts] = zero
    p_high[ghosts] = zero

    @pl.when(slab == 0)
    def _():
        p_low[...] = jnp.zeros_like(p_low)
        recv_c[1] = jnp.zeros(recv_c.shape[1:], recv_c.dtype)

    @pl.when(slab == slabs - 1)
    def _():
        p_high[...] = jnp.zeros_like(p_high)
        recv_c[0] = jnp.zeros(recv_c.shape[1:], recv_c.dtype)

    neighbours = stages + jnp.where(has_low, 1, 0) + jnp.where(has_high, 1, 0)
    pl.semaphore_wait(barrier, neighbours)
    copy_p[0].wait()

    halo_up = pltpu.make_async_remote_copy(
        src_ref=p_own.at[pl.ds((rows - GHOST) * kp, ghosts)],
        dst_ref=p_low.at[pl.ds(0, ghosts)],
        send_sem=halo_send.at[0], recv_sem=halo_recv.at[0],
        device_id=(slab + 1, me), device_id_type=MESH)
    halo_down = pltpu.make_async_remote_copy(
        src_ref=p_own.at[pl.ds(0, ghosts)],
        dst_ref=p_high.at[pl.ds(0, ghosts)],
        send_sem=halo_send.at[1], recv_sem=halo_recv.at[1],
        device_id=(slab - 1, me), device_id_type=MESH)

    @pl.when(has_high)
    def _():
        halo_up.start()

    for copy in copy_index:
        copy.wait()

    def find(n, base, none, which):
        row = jnp.clip(start - GHOST + n, 0, total - 1)
        place = []
        for m in range(kp):
            col = p_cols[me, m, row]
            near = col // coarse
            place.append((near - slab + 1) * coarse + slots[col % coarse, near])
        found = []
        for w in which:
            value = none
            for m in range(kp):
                value = jnp.where(place[m] == w, base + m, value)
            found.append(value)
        return found

    def at(i):
        return pl.ds(pl.multiple_of(i * block, block), block)

    middle = range(coarse, 2 * coarse)
    lower = range(0, coarse)
    upper = range(2 * coarse, 3 * coarse)
    q_at = {0: (q0, 0), 1: (q1, 0), 2: (q2, rows)}
    turned = {0: (qt0, 0), 1: (qt1, 0), 2: (qt2, rows - GHOST)}
    half = planes // 2

    def spread(first, count, which, blocks, offset, none, turn):
        def body(i, _):
            n = first + i
            found = find(n, (n - offset) * kp, none, which)
            for w, value in zip(which, found):
                j, slot = w // coarse, w % coarse
                q, before = q_at[j]
                piece = blocks[value]
                q[at(n - before), slot * block : (slot + 1) * block] = piece
                if turn:
                    qt, base = turned[j]
                    owner = slot // owned
                    low = (owner // 2) * owned * block + (slot % owned) * block
                    qt[owner % 2, low : low + block, at(n - GHOST - base)] = piece.T
            return 0

        lax.fori_loop(0, count, body, 0)

    for copy in copy_p[1:]:
        copy.wait()
    none = rows * kp
    spread(GHOST, GHOST, [*lower, *middle], p_own, GHOST, none, True)
    spread(2 * GHOST, rows - 2 * GHOST, [*middle], p_own, GHOST, none, True)
    spread(rows, GHOST, [*middle, *upper], p_own, GHOST, none, True)
    copy_a.wait()

    def place(first, count, low, high):
        def body(i, _):
            g = first + i
            local = [a_cols[k, 0, g] - (start - GHOST) for k in range(links)]
            for n in range(low, high):
                value = rows * links
                for k in range(links):
                    value = jnp.where(local[k] == n, g * links + k, value)
                piece = a_own[value]
                if n < GHOST:
                    dense_low[at(g), n * block : (n + 1) * block] = piece
                elif n < GHOST + rows:
                    dense[at(g), (n - GHOST) * block : (n - GHOST + 1) * block] = piece
                else:
                    m = n - GHOST - rows
                    dense_high[at(g - rows + GHOST), m * block : (m + 1) * block] = piece
            return 0

        lax.fori_loop(0, count, body, 0)

    place(0, GHOST, 0, GHOST + rows)
    place(GHOST, rows - 2 * GHOST, GHOST, GHOST + rows)
    place(rows - GHOST, GHOST, GHOST, rows + 2 * GHOST)

    gb = GHOST * block
    rb = rows * block
    bands = ((0, gb), (gb, rb - gb), (rb - gb, rb))
    inner = {0: (0, gb), 1: (0, rb), 2: (rb - gb, rb)}

    def own(band, c):
        first, last = bands[band]
        k0, k1 = inner[c]
        q, before = q_at[c]
        shift = gb - before * block
        keep = {(0, 0): 0, (0, 1): 1, (2, 1): 2, (2, 2): 3}.get((band, c))
        step = min(2 * block, last - first)
        for m in range(first, last, step):
            value = dot(dense[m : m + step, k0:k1], q[k0 + shift : k1 + shift, :])
            if keep is None:
                ap[c, m : m + step, :] = value.astype(bf)
            else:
                keep_ap[keep, m - first : m - first + step, :] = value

    def ghost(band, c):
        first, last = bands[band]
        q, before = q_at[c]
        left = dense_low if band == 0 else dense_high
        shift = (0 if band == 0 else gb + rb) - before * block
        keep = {(0, 0): 0, (0, 1): 1, (2, 1): 2, (2, 2): 3}[(band, c)]
        step = 2 * block
        for m in range(0, gb, step):
            value = dot(left[m : m + step, :], q[shift : shift + gb, :])
            ap[c, first + m : first + m + step, :] = (keep_ap[keep, m : m + step, :] + value).astype(bf)

    def stage_copy(t, j, c):
        return pltpu.make_async_remote_copy(
            src_ref=send_b[t].at[j, c], dst_ref=recv_b[t].at[j, c],
            send_sem=b_sem[t].at[j, c], recv_sem=b_got[t].at[j, c],
            device_id=(slab, partners[t]), device_id_type=MESH)

    def final_copy(j, c):
        return pltpu.make_async_remote_copy(
            src_ref=send_c.at[j, c], dst_ref=recv_c.at[j, c],
            send_sem=c_sem.at[j, c], recv_sem=c_got.at[j, c],
            device_id=(slab - 1 if j == 0 else slab + 1, me), device_id_type=MESH)

    parts = ((qt0, 0, gb), (qt1, 0, rb), (qt2, rb - gb, gb))
    shape = (half, owned * block, edge)

    def form(j, c):
        qt, first, depth = parts[j]
        right = ap[c, first : first + depth, :]
        send_b[0][j, c] = dot(qt[1 - bits[0]], right).astype(bf).reshape(shape)
        stage_copy(0, j, c).start()
        keep_b[0][j, c] = dot(qt[bits[0]], right).reshape(shape)

    def fold(j, c):
        for t in range(1, stages):
            stage_copy(t - 1, j, c).wait_recv()
            for i in range(planes >> (t + 1)):
                k = 1 - bits[t] + 2 * i
                send_b[t][j, c, i] = (
                    keep_b[t - 1][j, c, k] + recv_b[t - 1][j, c, k].astype(f32)).astype(bf)
            stage_copy(t, j, c).start()
            for i in range(planes >> (t + 1)):
                k = bits[t] + 2 * i
                keep_b[t][j, c, i] = keep_b[t - 1][j, c, k] + recv_b[t - 1][j, c, k].astype(f32)

    def finish(j, c):
        stage_copy(stages - 1, j, c).wait_recv()
        value = keep_b[stages - 1][j, c, 0] + recv_b[stages - 1][j, c, 0].astype(f32)
        if j == 1:
            final[c] = value
        else:
            send_c[j // 2, c] = value.astype(bf)

    def send(j, c):
        @pl.when(has_low if j == 0 else has_high)
        def _():
            final_copy(j // 2, c).start()

    own(0, 2)
    form(0, 2)
    own(2, 0)
    form(2, 0)
    own(0, 0)
    own(0, 1)
    fold(0, 2)
    fold(2, 0)
    own(1, 1)
    own(1, 0)
    own(1, 2)

    @pl.when(has_high)
    def _():
        halo_up.wait_send()

    @pl.when(has_low)
    def _():
        halo_down.start()

    own(2, 2)
    own(2, 1)

    @pl.when(has_low)
    def _():
        halo_up.wait_recv()

    spread(0, GHOST, [*lower, *middle], p_low, 0, ghosts, False)
    ghost(0, 0)
    form(0, 0)
    ghost(0, 1)
    form(0, 1)
    form(1, 0)
    fold(0, 0)
    fold(0, 1)
    fold(1, 0)
    finish(0, 2)
    finish(2, 0)
    finish(0, 0)

    @pl.when(has_low)
    def _():
        halo_down.wait_send()

    send(0, 2)
    send(2, 0)
    send(0, 0)
    finish(0, 1)
    send(0, 1)

    @pl.when(has_high)
    def _():
        halo_down.wait_recv()

    spread(GHOST + rows, GHOST, [*middle, *upper], p_high, GHOST + rows, ghosts, False)
    ghost(2, 1)
    form(2, 1)
    ghost(2, 2)
    form(2, 2)
    fold(2, 1)
    fold(2, 2)
    form(1, 2)
    form(1, 1)
    fold(1, 2)
    fold(1, 1)
    finish(2, 1)
    send(2, 1)
    finish(2, 2)
    send(2, 2)
    finish(1, 0)
    finish(1, 2)
    finish(1, 1)

    def out_copy(o):
        return pltpu.make_async_copy(whole.at[o], out.at[:, pl.ds(o * edge, edge)], out_sem.at[o])

    for o in (4, 3, 2, 1, 0):
        terms = []
        if 0 <= o - 1 < chunks:
            terms.append(final[o - 1])
        if o >= 2:
            @pl.when(has_high)
            def _():
                final_copy(0, o - 2).wait_recv()

            terms.append(recv_c[0, o - 2].astype(f32))
        if o < chunks:
            @pl.when(has_low)
            def _():
                final_copy(1, o).wait_recv()

            terms.append(recv_c[1, o].astype(f32))
        whole[o] = functools.reduce(jnp.add, terms)
        out_copy(o).start()

    @pl.when(has_high)
    def _():
        for c in range(chunks):
            final_copy(1, c).wait_send()

    @pl.when(has_low)
    def _():
        for c in range(chunks):
            final_copy(0, c).wait_send()

    for t in range(stages):
        for j in range(3):
            for c in range(chunks):
                stage_copy(t, j, c).wait_send()
    for o in range(5):
        out_copy(o).wait()


def on_device(a_blocks, a_cols, p_blocks, p_cols, coarse_slot):
    rows, links, block = a_blocks.shape[1:4]
    kp = p_blocks.shape[2]
    coarse = coarse_slot.shape[1]
    slabs = lax.axis_size("slab")
    planes = lax.axis_size("plane")
    owned = coarse // planes
    stages = planes.bit_length() - 1
    assert planes == 1 << stages and stages > 0 and rows >= 2 * GHOST
    edge = coarse * block
    high = owned * block
    dims = (slabs, planes, rows, links, kp, block, coarse, owned)
    bf, f32 = jnp.bfloat16, jnp.float32
    vmem = pltpu.VMEM
    dma = pltpu.SemaphoreType.DMA
    gb, rb = GHOST * block, rows * block
    shape = lambda t: (3, 3, planes >> (t + 1), high, edge)
    scratch = [
        vmem((rows * links + 1, block, block), bf),
        vmem((rows * kp + 1, block, block), bf),
        vmem((GHOST * kp + 1, block, block), bf),
        vmem((GHOST * kp + 1, block, block), bf),
        vmem((2 * gb, edge), bf),
        vmem((rb + 2 * gb, edge), bf),
        vmem((2 * gb, edge), bf),
        vmem((2, planes // 2 * high, gb), bf),
        vmem((2, planes // 2 * high, rb), bf),
        vmem((2, planes // 2 * high, gb), bf),
        vmem((rb, rb), bf),
        vmem((gb, gb), bf),
        vmem((gb, gb), bf),
        vmem((3, rb, edge), bf),
        vmem((4, gb, edge), f32),
        vmem((3, high, edge), f32),
        vmem((2, 3, high, edge), bf),
        vmem((2, 3, high, edge), bf),
        dma((4,)), dma((2,)), dma((2,)), dma((2, 3)), dma((2, 3)),
        vmem((5, high, edge), f32),
        dma((5,)),
        pltpu.SMEM((links, 1, rows), jnp.int32),
        pltpu.SMEM((planes, kp, p_cols.shape[1]), jnp.int32),
        pltpu.SMEM((coarse, slabs), jnp.int32),
        dma((3,)),
    ]
    scratch += [vmem(shape(t), bf) for t in range(stages)]
    scratch += [vmem(shape(t), bf) for t in range(stages)]
    scratch += [vmem(shape(t), f32) for t in range(stages)]
    scratch += [dma((3, 3)) for t in range(2 * stages)]
    outside = pl.BlockSpec(memory_space=pltpu.HBM)
    anywhere = pl.BlockSpec(memory_space=pl.ANY)
    result = pl.pallas_call(
        functools.partial(kernel, dims),
        out_shape=jax.ShapeDtypeStruct((high, 5 * edge), f32),
        in_specs=[outside] * 5,
        out_specs=anywhere,
        scratch_shapes=scratch,
        compiler_params=pltpu.CompilerParams(
            collective_id=0, has_side_effects=True, vmem_limit_bytes=50 * 1024 * 1024),
    )(*(pltpu.with_memory_space_constraint(x, pltpu.HBM) for x in (
        a_cols.transpose(2, 0, 1), p_cols.transpose(0, 2, 1), coarse_slot.T,
        a_blocks.reshape(rows * links, block, block), p_blocks.reshape(rows * kp, block, block))))
    return result.reshape(1, owned, block, 5 * edge)


def solution(mesh):
    return jax.shard_map(
        on_device,
        mesh=mesh,
        in_specs=(
            P("plane", "slab", None, None, None),
            P("plane", "slab", None),
            P("plane", "slab", None, None, None),
            P(),
            P(),
        ),
        out_specs=P("plane", "slab", None, None),
        check_vma=False,
    )
```

time: 54.1 us -> 47.8 us (0.88)
  the two profiles are of different devices: /device:TPU:0 before, /device:TPU:9 now
where the time goes in v1:
time: 47.8 us; the launch traced here: 47.7 us
  Pallas kernels  46.6 us (97%)
  local copies, waits for them, and re-layouts  1.06 us (2%)
    pallas_call x1, Pallas kernels, on_device(): pl.pallas_call(functools.partial(kernel, dims), out_shape=jax.ShapeDtypeS...  46.6 us
    unnamed x1, local copies, waits for them, and re-layouts  1.06 us

profile of v1, /device:TPU:9, one launch (start us, length us, event | category | flops | bytes accessed | tf_op | source)
XLA Modules:
  0.0 47.7 jit_solution(4093456205002471278)
XLA Ops:
  0.0 46.6 %shard_map.55 = f32[128,2560]{1,0:T(8,128)S(1)} custom-call(s32[7,1,12]{2,1,0:T(1,128)} %bitcast.10, s32[4,4,96]{2,1,0:T(4,128)} %bitcast.9, s32[4,8]{1,0:T(4,128)} %bitcast.11, bf16[84,128,128]{2,1,0:T(8,128)(2,1)} %bitcast.7, bf16[48,128,128]{2,1,0:T(8,128)(2,1)} %bitcast.8), custom_call_target="tpu_custom_call" | custom-call | tf_op jit(solution)/shard_map/pallas_call | solution.py:420
  46.6 1.1 %copy.7 = f32[1,1,128,2560]{3,2,1,0:T(8,128)} copy(f32[1,1,128,2560]{3,2,1,0:T(8,128)S(1)} %bitcast.6) | data formatting | bytes 2621440

commit v2 on v1

--- a/solution.py
+++ b/solution.py
@@ -19,30 +19,49 @@
     ghosts = GHOST * kp
     (a_own, p_own, p_low, p_high, q0, q1, q2, qt0, qt1, qt2, dense, dense_low, dense_high, ap, keep_ap, final,
      send_c, recv_c, local_sem, halo_send, halo_recv, c_sem, c_got, whole, out_sem, a_cols, p_cols, slots,
-     index_sem) = scratch[:29]
-    rest = scratch[29:]
+     index_sem, pass_p, pass_c, pass_sem, pass_got, pass_c_sem, pass_c_got) = scratch[:35]
+    rest = scratch[35:]
     send_b, recv_b, keep_b, b_sem, b_got = (rest[i * stages : (i + 1) * stages] for i in range(5))
     slab = lax.axis_index("slab")
     me = lax.axis_index("plane")
     bits = [(me // (1 << t)) % 2 for t in range(stages)]
     partners = [me + (1 - 2 * bits[t]) * (1 << t) for t in range(stages)]
-    has_low = slab > 0
-    has_high = slab < slabs - 1
     f32, bf = jnp.float32, jnp.bfloat16
     start = slab * rows
     total = p_cols.shape[2]
     dot = functools.partial(jnp.dot, preferred_element_type=f32)
+    turn = slab % 2
+    pairs = max(slabs // 2, 1)
+    level = slab // 2
+    first = slab - 1 + 2 * turn
+    second = slab + 1 - 2 * turn
+    past = slab + 2 - 4 * turn
+    has_first = (first >= 0) & (first < slabs)
+    has_second = second < slabs
+    has_past = (past >= 0) & (past < slabs) & has_second
+    far = jnp.where(has_second, jnp.where(turn == 0, level, pairs - 1 - level), 0)
+    near = jnp.where(turn == 0, pairs - 1 - level, level)
+    opening = turn * (rows - GHOST)
+    closing = (1 - turn) * (rows - GHOST)
+
+    def inner_row(i):
+        return jnp.where(i < GHOST, opening + i, jnp.where(i < rows - GHOST, i, closing + i - (rows - GHOST)))
+
+    def local_row(n):
+        low = jnp.where(turn == 0, n, rows + GHOST + n)
+        high = jnp.where(turn == 0, n, n - rows - GHOST)
+        return jnp.where(n < GHOST, low, jnp.where(n < GHOST + rows, GHOST + inner_row(n - GHOST), high))
 
     copy_index = [
         pltpu.make_async_copy(source, target, index_sem.at[i])
         for i, (source, target) in enumerate(
             ((a_cols_hbm, a_cols), (p_cols_hbm, p_cols), (slots_hbm, slots)))
     ]
-    spans = ((rows - GHOST, GHOST), (0, GHOST), (GHOST, rows - 2 * GHOST))
+    spans = ((opening, GHOST), (closing, GHOST), (GHOST, rows - 2 * GHOST))
     copy_p = [
         pltpu.make_async_copy(
-            p_hbm.at[pl.ds(first * kp, count * kp)], p_own.at[pl.ds(first * kp, count * kp)], local_sem.at[1 + i])
-        for i, (first, count) in enumerate(spans)
+            p_hbm.at[pl.ds(head * kp, count * kp)], p_own.at[pl.ds(head * kp, count * kp)], local_sem.at[1 + i])
+        for i, (head, count) in enumerate(spans)
     ]
     copy_a = pltpu.make_async_copy(a_hbm, a_own.at[pl.ds(0, rows * links)], local_sem.at[0])
     copy_p[0].start()
@@ -56,13 +75,11 @@
     for t in range(stages):
         pl.semaphore_signal(barrier, inc=1, device_id=(slab, partners[t]), device_id_type=MESH)
 
-    @pl.when(has_low)
-    def _():
-        pl.semaphore_signal(barrier, inc=1, device_id=(slab - 1, me), device_id_type=MESH)
-
-    @pl.when(has_high)
-    def _():
-        pl.semaphore_signal(barrier, inc=1, device_id=(slab + 1, me), device_id_type=MESH)
+    known = ((slab >= 1, slab - 1), (slab + 1 < slabs, slab + 1), (slab >= 2, slab - 2), (slab + 2 < slabs, slab + 2))
+    for exists, device in known:
+        @pl.when(exists)
+        def _():
+            pl.semaphore_signal(barrier, inc=1, device_id=(device, me), device_id_type=MESH)
 
     zero = jnp.zeros((block, block), bf)
     a_own[rows * links] = zero
@@ -70,45 +87,83 @@
     p_low[ghosts] = zero
     p_high[ghosts] = zero
 
-    @pl.when(slab == 0)
+    @pl.when(~has_first)
     def _():
         p_low[...] = jnp.zeros_like(p_low)
-        recv_c[1] = jnp.zeros(recv_c.shape[1:], recv_c.dtype)
-
-    @pl.when(slab == slabs - 1)
+        recv_c[0] = jnp.zeros(recv_c.shape[1:], recv_c.dtype)
+
+    @pl.when(~has_second)
     def _():
         p_high[...] = jnp.zeros_like(p_high)
-        recv_c[0] = jnp.zeros(recv_c.shape[1:], recv_c.dtype)
-
-    neighbours = stages + jnp.where(has_low, 1, 0) + jnp.where(has_high, 1, 0)
-    pl.semaphore_wait(barrier, neighbours)
+        recv_c[1] = jnp.zeros(recv_c.shape[1:], recv_c.dtype)
+
+    pl.semaphore_wait(barrier, stages + sum(jnp.where(exists, 1, 0) for exists, _ in known))
     copy_p[0].wait()
 
-    halo_up = pltpu.make_async_remote_copy(
-        src_ref=p_own.at[pl.ds((rows - GHOST) * kp, ghosts)],
-        dst_ref=p_low.at[pl.ds(0, ghosts)],
-        send_sem=halo_send.at[0], recv_sem=halo_recv.at[0],
-        device_id=(slab + 1, me), device_id_type=MESH)
-    halo_down = pltpu.make_async_remote_copy(
-        src_ref=p_own.at[pl.ds(0, ghosts)],
-        dst_ref=p_high.at[pl.ds(0, ghosts)],
-        send_sem=halo_send.at[1], recv_sem=halo_recv.at[1],
-        device_id=(slab - 1, me), device_id_type=MESH)
-
-    @pl.when(has_high)
-    def _():
-        halo_up.start()
+    sides = ((opening, p_low, first, has_first), (closing, p_high, second, has_second))
+
+    def through(k, i, units):
+        return i < k * units // pairs
+
+    def row_copy(o, i, relayed):
+        head, target, device, _ = sides[o]
+        return pltpu.make_async_remote_copy(
+            src_ref=p_own.at[pl.ds((head + i) * kp, kp)],
+            dst_ref=(pass_p if relayed else target).at[pl.ds(i * kp, kp)],
+            send_sem=halo_send.at[o, i], recv_sem=(pass_got.at[i] if relayed else halo_recv.at[o, i]),
+            device_id=(second if relayed else device, me), device_id_type=MESH)
+
+    def pass_copy(i):
+        return pltpu.make_async_remote_copy(
+            src_ref=pass_p.at[pl.ds(i * kp, kp)], dst_ref=p_low.at[pl.ds(i * kp, kp)],
+            send_sem=pass_sem.at[i], recv_sem=halo_recv.at[0, i],
+            device_id=(past, me), device_id_type=MESH)
+
+    def halo_start(o):
+        exists = sides[o][3]
+        for i in range(GHOST):
+            direct = exists
+            if o == 0 and i < GHOST - 1:
+                direct = exists & ~through(far, i, GHOST)
+
+                @pl.when(exists & through(far, i, GHOST))
+                def _():
+                    row_copy(o, i, True).start()
+
+            @pl.when(direct)
+            def _():
+                row_copy(o, i, False).start()
+
+    def halo_sent(o):
+        @pl.when(sides[o][3])
+        def _():
+            for i in range(GHOST):
+                row_copy(o, i, False).wait_send()
+
+    def halo_pass(i):
+        @pl.when(has_past & through(near, i, GHOST))
+        def _():
+            row_copy(0, i, True).wait_recv()
+            pass_copy(i).start()
+
+    def halo_wait(o):
+        @pl.when(sides[o][3])
+        def _():
+            for i in range(GHOST):
+                row_copy(o, i, False).wait_recv()
+
+    halo_start(0)
 
     for copy in copy_index:
         copy.wait()
 
     def find(n, base, none, which):
-        row = jnp.clip(start - GHOST + n, 0, total - 1)
+        row = jnp.clip(start - GHOST + local_row(n), 0, total - 1)
         place = []
         for m in range(kp):
             col = p_cols[me, m, row]
-            near = col // coarse
-            place.append((near - slab + 1) * coarse + slots[col % coarse, near])
+            ahead = col // coarse
+            place.append((1 + (ahead - slab) * (1 - 2 * turn)) * coarse + slots[col % coarse, ahead])
         found = []
         for w in which:
             value = none
@@ -127,16 +182,16 @@
     turned = {0: (qt0, 0), 1: (qt1, 0), 2: (qt2, rows - GHOST)}
     half = planes // 2
 
-    def spread(first, count, which, blocks, offset, none, turn):
+    def spread(head, count, which, blocks, none, flip):
         def body(i, _):
-            n = first + i
-            found = find(n, (n - offset) * kp, none, which)
+            n = head + i
+            found = find(n, (inner_row(n - GHOST) if flip else i) * kp, none, which)
             for w, value in zip(which, found):
                 j, slot = w // coarse, w % coarse
                 q, before = q_at[j]
                 piece = blocks[value]
                 q[at(n - before), slot * block : (slot + 1) * block] = piece
-                if turn:
+                if flip:
                     qt, base = turned[j]
                     owner = slot // owned
                     low = (owner // 2) * owned * block + (slot % owned) * block
@@ -148,19 +203,21 @@
     for copy in copy_p[1:]:
         copy.wait()
     none = rows * kp
-    spread(GHOST, GHOST, [*lower, *middle], p_own, GHOST, none, True)
-    spread(2 * GHOST, rows - 2 * GHOST, [*middle], p_own, GHOST, none, True)
-    spread(rows, GHOST, [*middle, *upper], p_own, GHOST, none, True)
+    spread(GHOST, GHOST, [*lower, *middle], p_own, none, True)
+    spread(2 * GHOST, rows - 2 * GHOST, [*middle], p_own, none, True)
+    spread(rows, GHOST, [*middle, *upper], p_own, none, True)
     copy_a.wait()
 
-    def place(first, count, low, high):
+    def place(head, count, low, high):
         def body(i, _):
-            g = first + i
-            local = [a_cols[k, 0, g] - (start - GHOST) for k in range(links)]
+            g = head + i
+            row = inner_row(g)
+            local = [a_cols[k, 0, row] - (start - GHOST) for k in range(links)]
             for n in range(low, high):
                 value = rows * links
+                at_n = local_row(n)
                 for k in range(links):
-                    value = jnp.where(local[k] == n, g * links + k, value)
+                    value = jnp.where(local[k] == at_n, row * links + k, value)
                 piece = a_own[value]
                 if n < GHOST:
                     dense_low[at(g), n * block : (n + 1) * block] = piece
@@ -183,21 +240,21 @@
     inner = {0: (0, gb), 1: (0, rb), 2: (rb - gb, rb)}
 
     def own(band, c):
-        first, last = bands[band]
+        head, last = bands[band]
         k0, k1 = inner[c]
         q, before = q_at[c]
         shift = gb - before * block
         keep = {(0, 0): 0, (0, 1): 1, (2, 1): 2, (2, 2): 3}.get((band, c))
-        step = min(2 * block, last - first)
-        for m in range(first, last, step):
+        step = min(2 * block, last - head)
+        for m in range(head, last, step):
             value = dot(dense[m : m + step, k0:k1], q[k0 + shift : k1 + shift, :])
             if keep is None:
                 ap[c, m : m + step, :] = value.astype(bf)
             else:
-                keep_ap[keep, m - first : m - first + step, :] = value
+                keep_ap[keep, m - head : m - head + step, :] = value
 
     def ghost(band, c):
-        first, last = bands[band]
+        head, last = bands[band]
         q, before = q_at[c]
         left = dense_low if band == 0 else dense_high
         shift = (0 if band == 0 else gb + rb) - before * block
@@ -205,7 +262,7 @@
         step = 2 * block
         for m in range(0, gb, step):
             value = dot(left[m : m + step, :], q[shift : shift + gb, :])
-            ap[c, first + m : first + m + step, :] = (keep_ap[keep, m : m + step, :] + value).astype(bf)
+            ap[c, head + m : head + m + step, :] = (keep_ap[keep, m : m + step, :] + value).astype(bf)
 
     def stage_copy(t, j, c):
         return pltpu.make_async_remote_copy(
@@ -213,18 +270,40 @@
             send_sem=b_sem[t].at[j, c], recv_sem=b_got[t].at[j, c],
             device_id=(slab, partners[t]), device_id_type=MESH)
 
-    def final_copy(j, c):
+    quarters = 4
+    slice_c = owned * block // quarters
+    order = (2, 0, 1)
+
+    def final_copy(o, c, h, relayed):
+        piece = pl.ds(h * slice_c, slice_c)
         return pltpu.make_async_remote_copy(
-            src_ref=send_c.at[j, c], dst_ref=recv_c.at[j, c],
-            send_sem=c_sem.at[j, c], recv_sem=c_got.at[j, c],
-            device_id=(slab - 1 if j == 0 else slab + 1, me), device_id_type=MESH)
+            src_ref=send_c.at[o, c, piece], dst_ref=(pass_c.at[c, piece] if relayed else recv_c.at[o, c, piece]),
+            send_sem=c_sem.at[o, c, h], recv_sem=(pass_c_got.at[c, h] if relayed else c_got.at[o, c, h]),
+            device_id=(second if relayed else sides[o][2], me), device_id_type=MESH)
+
+    def final_pass_copy(c, h):
+        piece = pl.ds(h * slice_c, slice_c)
+        return pltpu.make_async_remote_copy(
+            src_ref=pass_c.at[c, piece], dst_ref=recv_c.at[0, c, piece],
+            send_sem=pass_c_sem.at[c, h], recv_sem=c_got.at[0, c, h],
+            device_id=(past, me), device_id_type=MESH)
+
+    def final_through(k, c, h):
+        return through(k, order.index(c) * quarters + h, chunks * quarters)
+
+    def final_pass(c):
+        for h in range(quarters):
+            @pl.when(has_past & final_through(near, c, h))
+            def _():
+                final_copy(0, c, h, True).wait_recv()
+                final_pass_copy(c, h).start()
 
     parts = ((qt0, 0, gb), (qt1, 0, rb), (qt2, rb - gb, gb))
     shape = (half, owned * block, edge)
 
     def form(j, c):
-        qt, first, depth = parts[j]
-        right = ap[c, first : first + depth, :]
+        qt, head, depth = parts[j]
+        right = ap[c, head : head + depth, :]
         send_b[0][j, c] = dot(qt[1 - bits[0]], right).astype(bf).reshape(shape)
         stage_copy(0, j, c).start()
         keep_b[0][j, c] = dot(qt[bits[0]], right).reshape(shape)
@@ -250,75 +329,74 @@
             send_c[j // 2, c] = value.astype(bf)
 
     def send(j, c):
-        @pl.when(has_low if j == 0 else has_high)
-        def _():
-            final_copy(j // 2, c).start()
+        o = j // 2
+        exists = sides[o][3]
+        for h in range(quarters):
+            direct = exists
+            if o == 0:
+                direct = exists & ~final_through(far, c, h)
+
+                @pl.when(exists & final_through(far, c, h))
+                def _():
+                    final_copy(o, c, h, True).start()
+
+            @pl.when(direct)
+            def _():
+                final_copy(o, c, h, False).start()
 
     own(0, 2)
     form(0, 2)
     own(2, 0)
     form(2, 0)
+    halo_pass(0)
     own(0, 0)
     own(0, 1)
+    halo_pass(1)
     fold(0, 2)
     fold(2, 0)
     own(1, 1)
+    halo_sent(0)
+    halo_start(1)
     own(1, 0)
     own(1, 2)
-
-    @pl.when(has_high)
-    def _():
-        halo_up.wait_send()
-
-    @pl.when(has_low)
-    def _():
-        halo_down.start()
-
+    for i in range(2, GHOST - 1):
+        halo_pass(i)
     own(2, 2)
     own(2, 1)
-
-    @pl.when(has_low)
-    def _():
-        halo_up.wait_recv()
-
-    spread(0, GHOST, [*lower, *middle], p_low, 0, ghosts, False)
+    halo_wait(0)
+    spread(0, GHOST, [*lower, *middle], p_low, ghosts, False)
     ghost(0, 0)
     form(0, 0)
     ghost(0, 1)
     form(0, 1)
-    form(1, 0)
+    finish(0, 2)
+    finish(2, 0)
     fold(0, 0)
     fold(0, 1)
+    form(1, 0)
     fold(1, 0)
-    finish(0, 2)
-    finish(2, 0)
     finish(0, 0)
-
-    @pl.when(has_low)
-    def _():
-        halo_down.wait_send()
-
+    halo_sent(1)
     send(0, 2)
+    send(0, 0)
     send(2, 0)
-    send(0, 0)
-    finish(0, 1)
-    send(0, 1)
-
-    @pl.when(has_high)
-    def _():
-        halo_down.wait_recv()
-
-    spread(GHOST + rows, GHOST, [*middle, *upper], p_high, GHOST + rows, ghosts, False)
+    halo_wait(1)
+    spread(GHOST + rows, GHOST, [*middle, *upper], p_high, ghosts, False)
     ghost(2, 1)
     form(2, 1)
     ghost(2, 2)
     form(2, 2)
+    finish(0, 1)
+    send(0, 1)
     fold(2, 1)
     fold(2, 2)
     form(1, 2)
+    fold(1, 2)
     form(1, 1)
-    fold(1, 2)
+    final_pass(2)
     fold(1, 1)
+    final_pass(0)
+    final_pass(1)
     finish(2, 1)
     send(2, 1)
     finish(2, 2)
@@ -328,36 +406,41 @@
     finish(1, 1)
 
     def out_copy(o):
-        return pltpu.make_async_copy(whole.at[o], out.at[:, pl.ds(o * edge, edge)], out_sem.at[o])
-
-    for o in (4, 3, 2, 1, 0):
+        column = jnp.where(turn == 0, o, 4 - o) * edge
+        return pltpu.make_async_copy(whole.at[o], out.at[:, pl.ds(pl.multiple_of(column, edge), edge)], out_sem.at[o])
+
+    for o in (0, 1, 2, 4, 3):
         terms = []
         if 0 <= o - 1 < chunks:
             terms.append(final[o - 1])
-        if o >= 2:
-            @pl.when(has_high)
-            def _():
-                final_copy(0, o - 2).wait_recv()
-
-            terms.append(recv_c[0, o - 2].astype(f32))
-        if o < chunks:
-            @pl.when(has_low)
-            def _():
-                final_copy(1, o).wait_recv()
-
-            terms.append(recv_c[1, o].astype(f32))
+        for side, c in ((0, 2 - o), (1, 4 - o)):
+            if 0 <= c < chunks:
+                @pl.when(sides[side][3])
+                def _():
+                    for h in range(quarters):
+                        final_copy(side, c, h, False).wait_recv()
+
+                terms.append(recv_c[side, c].astype(f32))
         whole[o] = functools.reduce(jnp.add, terms)
         out_copy(o).start()
 
-    @pl.when(has_high)
-    def _():
-        for c in range(chunks):
-            final_copy(1, c).wait_send()
-
-    @pl.when(has_low)
-    def _():
-        for c in range(chunks):
-            final_copy(0, c).wait_send()
+    for o in range(2):
+        @pl.when(sides[o][3])
+        def _():
+            for c in range(chunks):
+                for h in range(quarters):
+                    final_copy(o, c, h, False).wait_send()
+
+    for i in range(GHOST - 1):
+        @pl.when(has_past & through(near, i, GHOST))
+        def _():
+            pass_copy(i).wait_send()
+
+    for c in range(chunks):
+        for h in range(quarters):
+            @pl.when(has_past & final_through(near, c, h))
+            def _():
+                final_pass_copy(c, h).wait_send()
 
     for t in range(stages):
         for j in range(3):
@@ -403,13 +486,16 @@
         vmem((3, high, edge), f32),
         vmem((2, 3, high, edge), bf),
         vmem((2, 3, high, edge), bf),
-        dma((4,)), dma((2,)), dma((2,)), dma((2, 3)), dma((2, 3)),
+        dma((4,)), dma((2, GHOST)), dma((2, GHOST)), dma((2, 3, 4)), dma((2, 3, 4)),
         vmem((5, high, edge), f32),
         dma((5,)),
         pltpu.SMEM((links, 1, rows), jnp.int32),
         pltpu.SMEM((planes, kp, p_cols.shape[1]), jnp.int32),
         pltpu.SMEM((coarse, slabs), jnp.int32),
         dma((3,)),
+        vmem(((GHOST - 1) * kp, block, block), bf),
+        vmem((3, high, edge), bf),
+        dma((GHOST - 1,)), dma((GHOST - 1,)), dma((3, 4)), dma((3, 4)),
     ]
     scratch += [vmem(shape(t), bf) for t in range(stages)]
     scratch += [vmem(shape(t), bf) for t in range(stages)]

time: 47.8 us -> 46.1 us (0.964)
  the two profiles are of different devices: /device:TPU:9 before, /device:TPU:21 now
where the time goes in v2:
time: 46.1 us; the launch traced here: 45.9 us
  Pallas kernels  44.9 us (97%)
  local copies, waits for them, and re-layouts  1.06 us (2%)
    pallas_call x1, Pallas kernels, on_device(): pl.pallas_call(functools.partial(kernel, dims), out_shape=jax.ShapeDtypeS...  44.9 us
    unnamed x1, local copies, waits for them, and re-layouts  1.06 us

profile of v2, /device:TPU:21, one launch (start us, length us, event | category | flops | bytes accessed | tf_op | source)
XLA Modules:
  0.0 45.9 jit_solution(1291841941101712268)
XLA Ops:
  0.0 44.9 %shard_map.55 = f32[128,2560]{1,0:T(8,128)S(1)} custom-call(s32[7,1,12]{2,1,0:T(1,128)} %bitcast.10, s32[4,4,96]{2,1,0:T(4,128)} %bitcast.9, s32[4,8]{1,0:T(4,128)} %bitcast.11, bf16[84,128,128]{2,1,0:T(8,128)(2,1)} %bitcast.7, bf16[48,128,128]{2,1,0:T(8,128)(2,1)} %bitcast.8), custom_call_target="tpu_custom_call" | custom-call | tf_op jit(solution)/shard_map/pallas_call | solution.py:506
  44.9 1.1 %copy.7 = f32[1,1,128,2560]{3,2,1,0:T(8,128)} copy(f32[1,1,128,2560]{3,2,1,0:T(8,128)S(1)} %bitcast.6) | data formatting | bytes 2621440

commit v3 on v2

--- a/solution.py
+++ b/solution.py
@@ -18,9 +18,9 @@
     chunks = 3
     ghosts = GHOST * kp
     (a_own, p_own, p_low, p_high, q0, q1, q2, qt0, qt1, qt2, dense, dense_low, dense_high, ap, keep_ap, final,
-     send_c, recv_c, local_sem, halo_send, halo_recv, c_sem, c_got, whole, out_sem, a_cols, p_cols, slots,
-     index_sem, pass_p, pass_c, pass_sem, pass_got, pass_c_sem, pass_c_got) = scratch[:35]
-    rest = scratch[35:]
+     send_c, recv_c, local_sem, halo_send, halo_recv, c_sem, c_got, a_cols, p_cols, slots,
+     index_sem, pass_p, pass_c, pass_sem, pass_got, pass_c_sem, pass_c_got, table) = scratch[:34]
+    rest = scratch[34:]
     send_b, recv_b, keep_b, b_sem, b_got = (rest[i * stages : (i + 1) * stages] for i in range(5))
     slab = lax.axis_index("slab")
     me = lax.axis_index("plane")
@@ -105,28 +105,32 @@
     def through(k, i, units):
         return i < k * units // pairs
 
+    units = 2 * GHOST
+    early = units - 2
+    piece_p = ghosts // units
+
     def row_copy(o, i, relayed):
         head, target, device, _ = sides[o]
         return pltpu.make_async_remote_copy(
-            src_ref=p_own.at[pl.ds((head + i) * kp, kp)],
-            dst_ref=(pass_p if relayed else target).at[pl.ds(i * kp, kp)],
+            src_ref=p_own.at[pl.ds(head * kp + i * piece_p, piece_p)],
+            dst_ref=(pass_p if relayed else target).at[pl.ds(i * piece_p, piece_p)],
             send_sem=halo_send.at[o, i], recv_sem=(pass_got.at[i] if relayed else halo_recv.at[o, i]),
             device_id=(second if relayed else device, me), device_id_type=MESH)
 
     def pass_copy(i):
         return pltpu.make_async_remote_copy(
-            src_ref=pass_p.at[pl.ds(i * kp, kp)], dst_ref=p_low.at[pl.ds(i * kp, kp)],
+            src_ref=pass_p.at[pl.ds(i * piece_p, piece_p)], dst_ref=p_low.at[pl.ds(i * piece_p, piece_p)],
             send_sem=pass_sem.at[i], recv_sem=halo_recv.at[0, i],
             device_id=(past, me), device_id_type=MESH)
 
     def halo_start(o):
         exists = sides[o][3]
-        for i in range(GHOST):
+        for i in range(units):
             direct = exists
-            if o == 0 and i < GHOST - 1:
-                direct = exists & ~through(far, i, GHOST)
-
-                @pl.when(exists & through(far, i, GHOST))
+            if o == 0 and i < units - 1:
+                direct = exists & ~through(far, i, units)
+
+                @pl.when(exists & through(far, i, units))
                 def _():
                     row_copy(o, i, True).start()
 
@@ -134,22 +138,24 @@
             def _():
                 row_copy(o, i, False).start()
 
-    def halo_sent(o):
+    def halo_sent(o, which):
         @pl.when(sides[o][3])
         def _():
-            for i in range(GHOST):
+            for i in which:
                 row_copy(o, i, False).wait_send()
 
-    def halo_pass(i):
-        @pl.when(has_past & through(near, i, GHOST))
+    def halo_pass(i, when=True):
+        @pl.when(has_past & through(near, i, units) & when)
         def _():
             row_copy(0, i, True).wait_recv()
             pass_copy(i).start()
 
+    most = 2 * near > pairs
+
     def halo_wait(o):
         @pl.when(sides[o][3])
         def _():
-            for i in range(GHOST):
+            for i in range(units):
                 row_copy(o, i, False).wait_recv()
 
     halo_start(0)
@@ -182,10 +188,21 @@
     turned = {0: (qt0, 0), 1: (qt1, 0), 2: (qt2, rows - GHOST)}
     half = planes // 2
 
+    def chart(o, head, which):
+        def body(i, _):
+            for k, value in enumerate(find(head + i, i * kp, ghosts, which)):
+                table[o, i, k] = value
+            return 0
+
+        lax.fori_loop(0, GHOST, body, 0)
+
     def spread(head, count, which, blocks, none, flip):
         def body(i, _):
             n = head + i
-            found = find(n, (inner_row(n - GHOST) if flip else i) * kp, none, which)
+            if flip:
+                found = find(n, inner_row(n - GHOST) * kp, none, which)
+            else:
+                found = [table[0 if head == 0 else 1, i, k] for k in range(len(which))]
             for w, value in zip(which, found):
                 j, slot = w // coarse, w % coarse
                 q, before = q_at[j]
@@ -289,7 +306,7 @@
             device_id=(past, me), device_id_type=MESH)
 
     def final_through(k, c, h):
-        return through(k, order.index(c) * quarters + h, chunks * quarters)
+        return through(k, order.index(c) * quarters + h, chunks * quarters) & (c != order[-1])
 
     def final_pass(c):
         for h in range(quarters):
@@ -344,25 +361,49 @@
             def _():
                 final_copy(o, c, h, False).start()
 
+    def write(o):
+        terms = []
+        if 0 <= o - 1 < chunks:
+            terms.append(final[o - 1])
+        for side, c in ((0, 2 - o), (1, 4 - o)):
+            if 0 <= c < chunks:
+                @pl.when(sides[side][3])
+                def _():
+                    for h in range(quarters):
+                        final_copy(side, c, h, False).wait_recv()
+
+                terms.append(recv_c[side, c].astype(f32))
+        column = jnp.where(turn == 0, o, 4 - o) * edge
+        out[:, pl.ds(pl.multiple_of(column, edge), edge)] = functools.reduce(jnp.add, terms)
+
     own(0, 2)
     form(0, 2)
     own(2, 0)
     form(2, 0)
-    halo_pass(0)
+    halo_pass(0, most)
     own(0, 0)
+    halo_pass(0, ~most)
     own(0, 1)
-    halo_pass(1)
+    halo_pass(1, most)
     fold(0, 2)
     fold(2, 0)
-    own(1, 1)
-    halo_sent(0)
-    halo_start(1)
     own(1, 0)
     own(1, 2)
-    for i in range(2, GHOST - 1):
-        halo_pass(i)
+    halo_pass(2, most)
+    own(1, 1)
+    halo_pass(3, most)
+    halo_sent(0, range(early))
+    halo_start(1)
+    halo_pass(1, ~most)
     own(2, 2)
     own(2, 1)
+    halo_pass(4, most)
+    chart(0, 0, [*lower, *middle])
+    halo_pass(2, ~most)
+    halo_pass(3, ~most)
+    halo_pass(4, ~most)
+    for i in range(5, units - 1):
+        halo_pass(i)
     halo_wait(0)
     spread(0, GHOST, [*lower, *middle], p_low, ghosts, False)
     ghost(0, 0)
@@ -375,54 +416,41 @@
     fold(0, 1)
     form(1, 0)
     fold(1, 0)
+    chart(1, GHOST + rows, [*middle, *upper])
+    halo_sent(0, range(early, units))
+    halo_sent(1, range(units))
+    send(0, 2)
+    send(2, 0)
     finish(0, 0)
-    halo_sent(1)
-    send(0, 2)
     send(0, 0)
-    send(2, 0)
     halo_wait(1)
     spread(GHOST + rows, GHOST, [*middle, *upper], p_high, ghosts, False)
     ghost(2, 1)
     form(2, 1)
     ghost(2, 2)
     form(2, 2)
+    fold(2, 1)
     finish(0, 1)
     send(0, 1)
-    fold(2, 1)
     fold(2, 2)
     form(1, 2)
     fold(1, 2)
     form(1, 1)
     final_pass(2)
     fold(1, 1)
-    final_pass(0)
-    final_pass(1)
     finish(2, 1)
     send(2, 1)
+    final_pass(0)
     finish(2, 2)
     send(2, 2)
     finish(1, 0)
+    write(0)
+    write(1)
+    write(4)
     finish(1, 2)
     finish(1, 1)
-
-    def out_copy(o):
-        column = jnp.where(turn == 0, o, 4 - o) * edge
-        return pltpu.make_async_copy(whole.at[o], out.at[:, pl.ds(pl.multiple_of(column, edge), edge)], out_sem.at[o])
-
-    for o in (0, 1, 2, 4, 3):
-        terms = []
-        if 0 <= o - 1 < chunks:
-            terms.append(final[o - 1])
-        for side, c in ((0, 2 - o), (1, 4 - o)):
-            if 0 <= c < chunks:
-                @pl.when(sides[side][3])
-                def _():
-                    for h in range(quarters):
-                        final_copy(side, c, h, False).wait_recv()
-
-                terms.append(recv_c[side, c].astype(f32))
-        whole[o] = functools.reduce(jnp.add, terms)
-        out_copy(o).start()
+    write(3)
+    write(2)
 
     for o in range(2):
         @pl.when(sides[o][3])
@@ -431,8 +459,8 @@
                 for h in range(quarters):
                     final_copy(o, c, h, False).wait_send()
 
-    for i in range(GHOST - 1):
-        @pl.when(has_past & through(near, i, GHOST))
+    for i in range(units - 1):
+        @pl.when(has_past & through(near, i, units))
         def _():
             pass_copy(i).wait_send()
 
@@ -446,8 +474,6 @@
         for j in range(3):
             for c in range(chunks):
                 stage_copy(t, j, c).wait_send()
-    for o in range(5):
-        out_copy(o).wait()
 
 
 def on_device(a_blocks, a_cols, p_blocks, p_cols, coarse_slot):
@@ -486,28 +512,26 @@
         vmem((3, high, edge), f32),
         vmem((2, 3, high, edge), bf),
         vmem((2, 3, high, edge), bf),
-        dma((4,)), dma((2, GHOST)), dma((2, GHOST)), dma((2, 3, 4)), dma((2, 3, 4)),
-        vmem((5, high, edge), f32),
-        dma((5,)),
+        dma((4,)), dma((2, 2 * GHOST)), dma((2, 2 * GHOST)), dma((2, 3, 4)), dma((2, 3, 4)),
         pltpu.SMEM((links, 1, rows), jnp.int32),
         pltpu.SMEM((planes, kp, p_cols.shape[1]), jnp.int32),
         pltpu.SMEM((coarse, slabs), jnp.int32),
         dma((3,)),
-        vmem(((GHOST - 1) * kp, block, block), bf),
+        vmem((GHOST * kp, block, block), bf),
         vmem((3, high, edge), bf),
-        dma((GHOST - 1,)), dma((GHOST - 1,)), dma((3, 4)), dma((3, 4)),
+        dma((2 * GHOST,)), dma((2 * GHOST,)), dma((3, 4)), dma((3, 4)),
+        pltpu.SMEM((2, GHOST, 2 * coarse), jnp.int32),
     ]
     scratch += [vmem(shape(t), bf) for t in range(stages)]
     scratch += [vmem(shape(t), bf) for t in range(stages)]
     scratch += [vmem(shape(t), f32) for t in range(stages)]
     scratch += [dma((3, 3)) for t in range(2 * stages)]
     outside = pl.BlockSpec(memory_space=pltpu.HBM)
-    anywhere = pl.BlockSpec(memory_space=pl.ANY)
     result = pl.pallas_call(
         functools.partial(kernel, dims),
         out_shape=jax.ShapeDtypeStruct((high, 5 * edge), f32),
         in_specs=[outside] * 5,
-        out_specs=anywhere,
+        out_specs=pl.BlockSpec(memory_space=pltpu.VMEM),
         scratch_shapes=scratch,
         compiler_params=pltpu.CompilerParams(
             collective_id=0, has_side_effects=True, vmem_limit_bytes=50 * 1024 * 1024),

time: 46.1 us -> 45.1 us (0.978)
  Pallas kernels: 44.9 us -> 43.9 us
    pallas_call x1, Pallas kernels: 44.9 us -> 43.9 us  [on_device(): pl.pallas_call(functools.partial(kernel, dims), out_shape=jax.ShapeDtypeS...]
where the time goes in v3:
time: 45.1 us; the launch traced here: 44.9 us
  Pallas kernels  43.9 us (97%)
  local copies, waits for them, and re-layouts  1.06 us (2%)
    pallas_call x1, Pallas kernels, on_device(): pl.pallas_call(functools.partial(kernel, dims), out_shape=jax.ShapeDtypeS...  43.9 us
    unnamed x1, local copies, waits for them, and re-layouts  1.06 us

profile of v3, /device:TPU:21, one launch (start us, length us, event | category | flops | bytes accessed | tf_op | source)
XLA Modules:
  0.0 44.9 jit_solution(1853914918837663281)
XLA Ops:
  0.0 43.9 %shard_map.55 = f32[128,2560]{1,0:T(8,128)S(1)} custom-call(s32[7,1,12]{2,1,0:T(1,128)} %bitcast.10, s32[4,4,96]{2,1,0:T(4,128)} %bitcast.9, s32[4,8]{1,0:T(4,128)} %bitcast.11, bf16[84,128,128]{2,1,0:T(8,128)(2,1)} %bitcast.7, bf16[48,128,128]{2,1,0:T(8,128)(2,1)} %bitcast.8), custom_call_target="tpu_custom_call" | custom-call | tf_op jit(solution)/shard_map/pallas_call | solution.py:530
  43.9 1.1 %copy.7 = f32[1,1,128,2560]{3,2,1,0:T(8,128)} copy(f32[1,1,128,2560]{3,2,1,0:T(8,128)S(1)} %bitcast.6) | data formatting | bytes 2621440

commit v4 on v3

--- a/solution.py
+++ b/solution.py
@@ -281,10 +281,10 @@
             value = dot(left[m : m + step, :], q[shift : shift + gb, :])
             ap[c, head + m : head + m + step, :] = (keep_ap[keep, m : m + step, :] + value).astype(bf)
 
-    def stage_copy(t, j, c):
+    def stage_copy(t, j, c, k):
         return pltpu.make_async_remote_copy(
-            src_ref=send_b[t].at[j, c], dst_ref=recv_b[t].at[j, c],
-            send_sem=b_sem[t].at[j, c], recv_sem=b_got[t].at[j, c],
+            src_ref=send_b[t].at[j, c, k], dst_ref=recv_b[t].at[j, c, k],
+            send_sem=b_sem[t].at[j, c, k], recv_sem=b_got[t].at[j, c, k],
             device_id=(slab, partners[t]), device_id_type=MESH)
 
     quarters = 4
@@ -318,27 +318,32 @@
     parts = ((qt0, 0, gb), (qt1, 0, rb), (qt2, rb - gb, gb))
     shape = (half, owned * block, edge)
 
+    tall = owned * block
+    picks = [1 - bits[1] + 2 * i for i in range(half // 2)] + [bits[1] + 2 * i for i in range(half // 2)]
+
     def form(j, c):
         qt, head, depth = parts[j]
         right = ap[c, head : head + depth, :]
         send_b[0][j, c] = dot(qt[1 - bits[0]], right).astype(bf).reshape(shape)
-        stage_copy(0, j, c).start()
+        for k in picks:
+            stage_copy(0, j, c, k).start()
         keep_b[0][j, c] = dot(qt[bits[0]], right).reshape(shape)
 
     def fold(j, c):
         for t in range(1, stages):
-            stage_copy(t - 1, j, c).wait_recv()
             for i in range(planes >> (t + 1)):
                 k = 1 - bits[t] + 2 * i
+                stage_copy(t - 1, j, c, k).wait_recv()
                 send_b[t][j, c, i] = (
                     keep_b[t - 1][j, c, k] + recv_b[t - 1][j, c, k].astype(f32)).astype(bf)
-            stage_copy(t, j, c).start()
+                stage_copy(t, j, c, i).start()
             for i in range(planes >> (t + 1)):
                 k = bits[t] + 2 * i
+                stage_copy(t - 1, j, c, k).wait_recv()
                 keep_b[t][j, c, i] = keep_b[t - 1][j, c, k] + recv_b[t - 1][j, c, k].astype(f32)
 
     def finish(j, c):
-        stage_copy(stages - 1, j, c).wait_recv()
+        stage_copy(stages - 1, j, c, 0).wait_recv()
         value = keep_b[stages - 1][j, c, 0] + recv_b[stages - 1][j, c, 0].astype(f32)
         if j == 1:
             final[c] = value
@@ -378,28 +383,28 @@
 
     own(0, 2)
     form(0, 2)
+    halo_pass(0, most)
     own(2, 0)
     form(2, 0)
-    halo_pass(0, most)
+    halo_pass(1, most)
+    halo_pass(0, ~most)
     own(0, 0)
-    halo_pass(0, ~most)
     own(0, 1)
-    halo_pass(1, most)
+    halo_pass(2, most)
     fold(0, 2)
     fold(2, 0)
     own(1, 0)
-    own(1, 2)
-    halo_pass(2, most)
-    own(1, 1)
     halo_pass(3, most)
+    halo_pass(1, ~most)
     halo_sent(0, range(early))
     halo_start(1)
-    halo_pass(1, ~most)
+    own(1, 2)
+    own(1, 1)
+    halo_pass(4, most)
+    halo_pass(2, ~most)
     own(2, 2)
     own(2, 1)
-    halo_pass(4, most)
     chart(0, 0, [*lower, *middle])
-    halo_pass(2, ~most)
     halo_pass(3, ~most)
     halo_pass(4, ~most)
     for i in range(5, units - 1):
@@ -473,7 +478,8 @@
     for t in range(stages):
         for j in range(3):
             for c in range(chunks):
-                stage_copy(t, j, c).wait_send()
+                for k in range(planes >> (t + 1)):
+                    stage_copy(t, j, c, k).wait_send()
 
 
 def on_device(a_blocks, a_cols, p_blocks, p_cols, coarse_slot):
@@ -484,7 +490,7 @@
     planes = lax.axis_size("plane")
     owned = coarse // planes
     stages = planes.bit_length() - 1
-    assert planes == 1 << stages and stages > 0 and rows >= 2 * GHOST
+    assert planes == 1 << stages and stages > 1 and rows >= 2 * GHOST
     edge = coarse * block
     high = owned * block
     dims = (slabs, planes, rows, links, kp, block, coarse, owned)
@@ -525,7 +531,7 @@
     scratch += [vmem(shape(t), bf) for t in range(stages)]
     scratch += [vmem(shape(t), bf) for t in range(stages)]
     scratch += [vmem(shape(t), f32) for t in range(stages)]
-    scratch += [dma((3, 3)) for t in range(2 * stages)]
+    scratch += [dma(shape(t % stages)[:3]) for t in range(2 * stages)]
     outside = pl.BlockSpec(memory_space=pltpu.HBM)
     result = pl.pallas_call(
         functools.partial(kernel, dims),

time: 45.1 us -> 44.2 us (0.980)
  Pallas kernels: 43.9 us -> 43 us
    pallas_call x1, Pallas kernels: 43.9 us -> 43 us  [on_device(): pl.pallas_call(functools.partial(kernel, dims), out_shape=jax.ShapeDtypeS...]
where the time goes in v4:
time: 44.2 us; the launch traced here: 44.1 us
  Pallas kernels  43 us (97%)
  local copies, waits for them, and re-layouts  1.06 us (2%)
    pallas_call x1, Pallas kernels, on_device(): pl.pallas_call(functools.partial(kernel, dims), out_shape=jax.ShapeDtypeS...  43 us
    unnamed x1, local copies, waits for them, and re-layouts  1.06 us

profile of v4, /device:TPU:21, one launch (start us, length us, event | category | flops | bytes accessed | tf_op | source)
XLA Modules:
  0.0 44.1 jit_solution(5386904254011405896)
XLA Ops:
  0.0 43.0 %shard_map.55 = f32[128,2560]{1,0:T(8,128)S(1)} custom-call(s32[7,1,12]{2,1,0:T(1,128)} %bitcast.10, s32[4,4,96]{2,1,0:T(4,128)} %bitcast.9, s32[4,8]{1,0:T(4,128)} %bitcast.11, bf16[84,128,128]{2,1,0:T(8,128)(2,1)} %bitcast.7, bf16[48,128,128]{2,1,0:T(8,128)(2,1)} %bitcast.8), custom_call_target="tpu_custom_call" | custom-call | tf_op jit(solution)/shard_map/pallas_call | solution.py:536
  43.0 1.1 %copy.7 = f32[1,1,128,2560]{3,2,1,0:T(8,128)} copy(f32[1,1,128,2560]{3,2,1,0:T(8,128)S(1)} %bitcast.6) | data formatting | bytes 2621440
